TPU v7x, 32 devices: a whole 2x2x4 slice. The times are simulated.
32 devices in a mesh: space: 16 (over z, y, core), tensor: 2 (over x).
Axes of the slice: x: 2, y: 2, z: 4, core: 2. Of those that a mesh axis runs over, the one named last changes fastest.
Arguments:
- tokens: bfloat16 [14336, 1024], P('space', 'tensor'), may hold values from -6 to 6
- first_weight: bfloat16 [1024, 1024], P(None, 'tensor'), may hold values from -0.1875 to 0.1875
- second_weight: bfloat16 [1024, 1024], P(None, 'tensor'), may hold values from -0.1875 to 0.1875
- head_weight: bfloat16 [352, 1024], P('tensor'), may hold values from -0.1875 to 0.1875
- targets: float32 [352, 14336], P('tensor', 'space'), may hold values from -6 to 6
- land_mask: int32 [4, 14336], P(None, 'space'), may hold values from 0 to 1, as said below
- variable_kind: int32 [88], P('tensor'), may hold values from 0 to 2
- loss_scale: float32 [], replicated, may hold values from 630784 to 5046272
Outputs:
- loss: float32 [], replicated
- token_grad: float32 [14336, 1024], P('space', 'tensor')
- first_grad: float32 [1024, 1024], P('space', 'tensor')
- second_grad: float32 [1024, 1024], P('space', 'tensor')
- head_grad: float32 [352, 1024], P('tensor', 'space')
Inputs may be any that keep to these rules, and one draw needn't show every extreme that they name: `land_mask`: every aligned group of 8 entries along the last dimension holds at least one 1 and one 0. `variable_kind`: 0 scores a variable on all cells, 1 on land cells, 2 on ocean cells.
All inputs are finite; a program needn't handle non-finite values.
Results may differ from a plain program's by a relative error of at most 0.0056.
Values may be sent and summed in bfloat16 or wider, within the bound.
A program may use at most 64 MiB of HBM per device.

v0:
```python
import math
import jax
import jax.numpy as jnp
from jax import lax
from jax.sharding import PartitionSpec as P

V = 88
PP = 4
PROW_DEV = 4
LONP = 224


def slope(z):
    cdf = 0.5 * (1.0 + lax.erf(z / math.sqrt(2.0)))
    return cdf + z * jnp.exp(-0.5 * z * z) / math.sqrt(2.0 * math.pi)


def column_folder(weights, piece):
    return lax.dot_general(
        piece, weights, (((1,), (1,)), ((), ())), preferred_element_type=jnp.float32
    )


def row_folder(weights, piece):
    return lax.dot_general(
        piece, weights, (((0,), (0,)), ((), ())), preferred_element_type=jnp.float32
    )


def per_device(
    tokens, first_weight, second_weight, head_weight, targets, land_mask, variable_kind, loss_scale
):
    count = tokens.shape[0]
    width = first_weight.shape[1]
    kinds = head_weight.shape[0] // PP
    rows_first, rows_second = (
        lax.all_to_all(first_weight, "tensor", split_axis=0, concat_axis=1, tiled=True),
        lax.all_to_all(second_weight, "tensor", split_axis=0, concat_axis=1, tiled=True),
    )
    head_cols = lax.all_to_all(head_weight, "tensor", split_axis=1, concat_axis=0, tiled=True)
    position = lax.axis_index("space") * count + jnp.arange(count, dtype=jnp.int32)
    cell = jnp.arange(PP, dtype=jnp.int32)
    lat_row = 2 * (position // LONP)[None, :] + (cell // 2)[:, None]
    nlat = 2 * PROW_DEV * lax.axis_size("space")
    cell_weight = jnp.cos(math.pi / 2.0 * (lat_row.astype(jnp.float32) + 0.5) / nlat)
    land = land_mask.astype(jnp.float32)
    kind = variable_kind[:, None, None]
    valid = jnp.where(kind == 0, 1.0, jnp.where(kind == 1, land[None], 1.0 - land[None]))
    masked = cell_weight[None] * valid
    local_weight = jnp.sum(masked, axis=(1, 2))
    weight_sum = lax.psum(local_weight, "space")
    full_in = lax.all_gather(tokens, "tensor", axis=1, tiled=True)
    pre_one = jnp.dot(full_in, first_weight, preferred_element_type=jnp.float32)
    hidden_one = jax.nn.gelu(pre_one, approximate=False).astype(jnp.bfloat16)
    full_one = lax.all_gather(hidden_one, "tensor", axis=1, tiled=True)
    pre_two = jnp.dot(full_one, second_weight, preferred_element_type=jnp.float32)
    hidden_two = jax.nn.gelu(pre_two, approximate=False).astype(jnp.bfloat16)
    full_two = lax.all_gather(hidden_two, "tensor", axis=1, tiled=True)
    predicted = lax.dot_general(
        head_weight, full_two, (((1,), (1,)), ((), ())), preferred_element_type=jnp.float32
    )
    error = predicted.reshape(kinds, PP, count) - targets.reshape(kinds, PP, count)
    local_error = jnp.sum(masked * error * error, axis=(1, 2))
    error_sum = lax.psum(local_error, "space")
    root = jnp.sqrt(error_sum / weight_sum + 1e-06)
    loss = lax.psum(jnp.sum(root), "tensor") / V
    coef = loss_scale / (V * root * weight_sum)
    grad_pred = (
        (coef[:, None, None] * masked * error).reshape(kinds * PP, count).astype(jnp.bfloat16)
    )
    back_two = row_folder(head_cols, lax.all_gather(grad_pred, "tensor", axis=0, tiled=True))
    head_term = jnp.dot(grad_pred, full_two, preferred_element_type=jnp.float32)
    head_grad = lax.psum_scatter(head_term, "space", scatter_dimension=1, tiled=True)
    grad_two = (back_two * slope(pre_two)).astype(jnp.bfloat16)
    back_one = column_folder(rows_second, lax.all_gather(grad_two, "tensor", axis=1, tiled=True))
    grad_one = (back_one * slope(pre_one)).astype(jnp.bfloat16)
    joined = lax.psum_scatter(
        jnp.concatenate(
            [
                lax.dot_general(
                    full_one, grad_two, (((0,), (0,)), ((), ())), preferred_element_type=jnp.float32
                ),
                lax.dot_general(
                    full_in, grad_one, (((0,), (0,)), ((), ())), preferred_element_type=jnp.float32
                ),
            ],
            axis=1,
        ),
        "space",
        scatter_dimension=0,
        tiled=True,
    )
    second_grad = joined[:, :width]
    first_grad = joined[:, width:]
    token_grad = column_folder(rows_first, lax.all_gather(grad_one, "tensor", axis=1, tiled=True))
    return (loss, token_grad, first_grad, second_grad, head_grad)


def solution(mesh):
    return jax.shard_map(
        per_device,
        mesh=mesh,
        in_specs=(
            P("space", "tensor"),
            P(None, "tensor"),
            P(None, "tensor"),
            P("tensor", None),
            P("tensor", "space"),
            P(None, "space"),
            P("tensor"),
            P(),
        ),
        out_specs=(
            P(),
            P("space", "tensor"),
            P("space", "tensor"),
            P("space", "tensor"),
            P("tensor", "space"),
        ),
        check_vma=False,
    )
```

profile of v0, /device:TPU:0, one launch (start us, length us, event | category | flops | bytes accessed | tf_op | source)
XLA Modules:
  0.0 390.4 jit_solution(11387166332372937541)
XLA Ops:
  7.2 0.7 all-gather.6.cloned.1.call-update
  8.0 34.5 %all-gather.6.cloned.1.call-done = bf16[896,1024]{1,0:T(8,128)(2,1)} async-done(((bf16[896,512]{1,0:T(8,128)(2,1)}), bf16[896,1024]{1,0:T(8,128)(2,1)}) %all-gather.6.cloned.1.call-update) | async-done | bytes 1835024 | tf_op jit(solution)/shard_map/all_gather | solution.py:52
  42.4 8.0 %fusion.2 = (bf16[896,512]{1,0:T(8,128)(2,1)}, f32[896,512]{1,0:T(8,128)}) fusion(bf16[896,1024]{1,0:T(8,128)(2,1)} %all-gather.6.cloned.1.call-done, bf16[1024,512]{1,0:T(8,128)(2,1)} %param.9), kind=kOutput, calls=%fused_computation.7 | convolution fusion | flops 969342976 | bytes 5636096 | tf_op jit(solution)/shard_map/dot_general | solution.py:53
  50.5 30.2 %all-gather.8.cloned.1.call-done = bf16[896,1024]{1,0:T(8,128)(2,1)} async-done(((bf16[896,512]{1,0:T(8,128)(2,1)}), bf16[896,1024]{1,0:T(8,128)(2,1)}) %all-gather.8.cloned.1.call-update) | async-done | bytes 1835024 | tf_op jit(solution)/shard_map/all_gather | solution.py:55
  80.7 7.5 %fusion.5 = (bf16[896,512]{1,0:T(8,128)(2,1)}, f32[896,512]{1,0:T(8,128)}) fusion(bf16[896,1024]{1,0:T(8,128)(2,1)} %all-gather.8.cloned.1.call-done, bf16[1024,512]{1,0:T(8,128)(2,1)S(1)} %copy-done.4), kind=kOutput, calls=%fused_computation.10 | convolution fusion | flops 969342976 | bytes 5636096 | tf_op jit(solution)/shard_map/dot_general | solution.py:56
  88.2 0.8 copy.33
  89.0 4.2 %all-to-all-start = ((bf16[176,2,512]{2,0,1:T(8,128)(2,1)}), bf16[176,2,512]{2,0,1:T(8,128)(2,1)}, u32[]{:S(2)}, u32[]{:S(2)}) async-start(bf16[176,2,512]{2,0,1:T(8,128)(2,1)} %bitcast.37), calls=%async_computation | async-start | bytes 720896 | tf_op jit(solution)/shard_map/all_to_all | solution.py:40
  93.6 0.2 mul.117
  95.5 0.8 multiply_reduce_fusion
  96.3 23.1 %all-gather.10.cloned.1.call-done = bf16[896,1024]{1,0:T(8,128)(2,1)} async-done(((bf16[896,512]{1,0:T(8,128)(2,1)}), bf16[896,1024]{1,0:T(8,128)(2,1)}) %all-gather.10.cloned.1.call-update) | async-done | bytes 1835024 | tf_op jit(solution)/shard_map/all_gather | solution.py:58
  119.4 2.6 fusion.33
  122.2 33.2 %all-reduce = (f32[44]{0:T(128)S(1)}, f32[44]{0:T(128)S(1)}) all-reduce(f32[44]{0:T(128)S(1)} %reduce_sum.36, f32[44]{0:T(128)S(1)} %multiply_reduce_fusion), channel_id=1, replica_groups=mesh['space'=16,'tensor'=2] {'space'}, use_global_device_ids=true, to_apply=%region_2.3 | all-reduce | flops 88 | bytes 704 | tf_op jit(solution)/shard_map/psum | solution.py:64
  155.8 7.6 %all_gather.21 = bf16[352,896]{1,0:T(8,128)(2,1)S(1)} all-gather(bf16[176,896]{1,0:T(8,128)(2,1)S(1)} %multiply_convert_fusion), channel_id=1, replica_groups=mesh['space'=16,'tensor'=2] {'tensor'}, dimensions={0}, use_global_device_ids=true | all-gather | bytes 946176 | tf_op jit(solution)/shard_map/all_gather | solution.py:71
  163.4 3.7 fusion.11
  167.2 22.7 %all_to_all.57 = bf16[2,512,512]{2,1,0:T(8,128)(2,1)S(1)} all-to-all(bf16[2,512,512]{2,1,0:T(8,128)(2,1)S(1)} %bitcast.41), channel_id=1, replica_groups=mesh['space'=16,'tensor'=2] {'tensor'}, dimensions={0} | all-to-all | bytes 2097152 | tf_op jit(solution)/shard_map/all_to_all | solution.py:38
  189.9 0.5 copy.23
  190.4 8.6 %all-gather.12.cloned.1.call-done = bf16[896,1024]{1,0:T(8,128)(2,1)} async-done(((bf16[896,512]{1,0:T(8,128)(2,1)}), bf16[896,1024]{1,0:T(8,128)(2,1)}) %all-gather.12.cloned.1.call-update) | async-done | bytes 1835024 | tf_op jit(solution)/shard_map/all_gather | solution.py:75
  199.0 4.6 %fusion.17 = bf16[896,512]{1,0:T(8,128)(2,1)} fusion(f32[896,512]{1,0:T(8,128)} %get-tuple-element.36, bf16[896,1024]{1,0:T(8,128)(2,1)} %all-gather.12.cloned.1.call-done, bf16[512,1024]{0,1:T(8,128)(2,1)S(1)} %bitcast.44), kind=kOutput, calls=%fused_computation.22 | convolution fusion | flops 944111616 | bytes 5636096 | tf_op jit(solution)/shard_map/dot_general | solution.py:19
  203.7 3.2 fusion.38
  206.8 1.3 convolution_bitcast_fusion
  208.1 2.5 pad_maximum_fusion
  210.6 5.5 %copy.27 = f32[1024,1024]{1,0:T(8,128)} copy(f32[1024,1024]{0,1:T(8,128)} %pad_maximum_fusion) | data formatting | bytes 8388608
  216.2 3.7 all-to-all-start.2
  220.0 1.9 fusion.39
  221.9 0.6 reduce_sum.38
  222.5 22.4 %all-to-all-done.2 = bf16[2,512,512]{2,1,0:T(8,128)(2,1)S(1)} async-done(((bf16[2,512,512]{2,1,0:T(8,128)(2,1)}), bf16[2,512,512]{2,1,0:T(8,128)(2,1)S(1)}, u32[]{:S(2)}, u32[]{:S(2)}) %all-to-all-start.2) | async-done | bytes 1048608 | tf_op jit(solution)/shard_map/all_to_all | solution.py:37
  244.9 0.5 copy.24
  245.4 5.6 %psum.23 = f32[]{:T(128)} all-reduce(f32[]{:T(128)} %reduce_sum.38), channel_id=1, replica_groups=mesh['space'=16,'tensor'=2] {'tensor'}, use_global_device_ids=true, to_apply=%region_6.7 | all-reduce | flops 1 | bytes 8 | tf_op jit(solution)/shard_map/psum | solution.py:66
  251.7 3.9 fusion.37
  255.5 66.0 %reduce-scatter.7.cloned.1.call-done = f32[64,1024]{1,0:T(8,128)} async-done(((f32[1024,1024]{1,0:T(8,128)}), f32[64,1024]{1,0:T(8,128)}) %reduce-scatter.7.cloned.1.call-update) | async-done | bytes 262160
  321.5 1.7 fusion.36
  323.2 59.2 %reduce-scatter.5.cloned.1.call-done = f32[176,64]{0,1:T(8,128)} async-done(((f32[176,1024]{0,1:T(8,128)}), f32[176,64]{0,1:T(8,128)}) %reduce-scatter.5.cloned.1.call-update) | async-done | bytes 45072 | tf_op jit(solution)/shard_map/reduce_scatter | solution.py:73
  (51 shorter events, 2.3 us)
Async XLA Ops:
  7.2 35.2 %all-gather.6.cloned.1.call-start = ((), (), s32[]{:S(2)}) async-start(), calls=%async_computation.5 | async-start | bytes 2752512 | tf_op jit(solution)/shard_map/all_gather | solution.py:52
  7.9 72.8 %copy-start.4 = (bf16[1024,512]{1,0:T(8,128)(2,1)S(1)}, bf16[1024,512]{1,0:T(8,128)(2,1)}, u32[]{:S(2)}) copy-start(bf16[1024,512]{1,0:T(8,128)(2,1)} %param.10) | copy-start | bytes 3145732
  7.9 72.8 %all-gather.8.cloned.1.call-start = ((), (), s32[]{:S(2)}) async-start(), calls=%async_computation.6 | async-start | bytes 2752512 | tf_op jit(solution)/shard_map/all_gather | solution.py:55
  50.4 37.8 %copy-start.3 = (bf16[176,1024]{1,0:T(8,128)(2,1)S(1)}, bf16[176,1024]{1,0:T(8,128)(2,1)}, u32[]{:S(2)}) copy-start(bf16[176,1024]{1,0:T(8,128)(2,1)} %param.11) | copy-start | bytes 1081348
  50.4 69.0 %all-gather.10.cloned.1.call-start = ((), (), s32[]{:S(2)}) async-start(), calls=%async_computation.7 | async-start | bytes 2752512 | tf_op jit(solution)/shard_map/all_gather | solution.py:58
  88.2 5.0 %copy-start.6 = (s32[4,896]{1,0:T(4,128)S(1)}, s32[4,896]{1,0:T(4,128)}, u32[]{:S(2)}) copy-start(s32[4,896]{1,0:T(4,128)} %param.13) | copy-start | bytes 43012
  89.0 74.4 %all-to-all-start = ((bf16[176,2,512]{2,0,1:T(8,128)(2,1)}), bf16[176,2,512]{2,0,1:T(8,128)(2,1)}, u32[]{:S(2)}, u32[]{:S(2)}) async-start(bf16[176,2,512]{2,0,1:T(8,128)(2,1)} %bitcast.37), calls=%async_computation | async-start | bytes 720896 | tf_op jit(solution)/shard_map/all_to_all | solution.py:40
  93.2 105.8 %all-gather.12.cloned.1.call-start = ((), (), s32[]{:S(2)}) async-start(), calls=%async_computation.8 | async-start | bytes 2752512 | tf_op jit(solution)/shard_map/all_gather | solution.py:75
  93.8 0.7 copy-start.7
  163.4 3.8 copy-start.5
  167.2 84.5 %all-gather.14.cloned.1.call-start = ((), (), s32[]{:S(2)}) async-start(), calls=%async_computation.9 | async-start | bytes 2752512 | tf_op jit(solution)/shard_map/all_gather | solution.py:95
  203.6 3.2 copy-start.1
  203.6 3.2 copy-start.2
  203.6 117.9 %reduce-scatter.7.cloned.1.call-start = ((), (), s32[]{:S(2)}) async-start(), calls=%async_computation.11 | async-start | bytes 4456448
  216.2 3.8 copy-start
  216.2 28.7 %all-to-all-start.2 = ((bf16[2,512,512]{2,1,0:T(8,128)(2,1)}), bf16[2,512,512]{2,1,0:T(8,128)(2,1)S(1)}, u32[]{:S(2)}, u32[]{:S(2)}) async-start(bf16[2,512,512]{2,1,0:T(8,128)(2,1)} %bitcast.42), calls=%async_computation.2 | async-start | bytes 2097152 | tf_op jit(solution)/shard_map/all_to_all | solution.py:37
  219.9 162.5 %reduce-scatter.5.cloned.1.call-start = ((), (), s32[]{:S(2)}) async-start(), calls=%async_computation.10 | async-start | bytes 1114112 | tf_op jit(solution)/shard_map/reduce_scatter | solution.py:73
Sparse Core Ops, SparseCore 0:
  9.5 32.8 all-gather.5
  50.5 30.1 all-gather.7
  88.3 31.0 all-gather.9
  167.3 31.6 all-gather.11
  203.7 40.9 all-gather.13
  248.5 72.9 reduce-scatter.6
  325.7 56.6 reduce-scatter.4
where the time goes:
time: 391 us; the launch traced here: 390 us
  waiting for transfers between devices  245 us (63%)
  blocking collectives  69.1 us (18%)
  matrix products  36.5 us (9%)
  between operations  16.8 us (4%)
  local copies, waits for them, and re-layouts  10.7 us (3%)
  starting transfers between devices  8.16 us (2%)
  other arithmetic  4.37 us (1%)
    unnamed x8, waiting for transfers between devices  66.7 us
    reduce_scatter x1, waiting for transfers between devices, per_device(): lax.psum_scatter(head_term, 'space', scatter_dimension=1, tiled=True)  59.2 us
    all_gather x1, waiting for transfers between devices, per_device(): full_in = lax.all_gather(tokens, 'tensor', axis=1, tiled=True)  34.5 us
    psum x1, blocking collectives, per_device(): error_sum = lax.psum(local_error, 'space')  33.2 us
    all_gather x1, waiting for transfers between devices, per_device(): full_one = lax.all_gather(hidden_one, 'tensor', axis=1, tiled=True)  30.2 us
    all_gather x1, waiting for transfers between devices, per_device(): full_two = lax.all_gather(hidden_two, 'tensor', axis=1, tiled=True)  23.1 us
    all_to_all x1, blocking collectives, per_device(): lax.all_to_all(second_weight, 'tensor', split_axis=0, concat_axis=1, tile...  22.7 us
    all_to_all x1, waiting for transfers between devices, per_device(): lax.all_to_all(first_weight, 'tensor', split_axis=0, concat_axis=1, tiled...  22.4 us
  transfers between devices with their start and end apart: 9, of which 7 were waited for; matrix products, arithmetic and copies ran while one was open for 7% of the time, Pallas kernels for 0%

commit v1 on v0

--- a/solution.py
+++ b/solution.py
@@ -8,6 +8,15 @@
 PP = 4
 PROW_DEV = 4
 LONP = 224
+balance_ports = lambda point, device_axis: jnp.concatenate(
+    lax.all_to_all(
+        jnp.stack(jnp.split(point, lax.axis_size(device_axis), axis=0)),
+        axis_name=device_axis,
+        split_axis=0,
+        concat_axis=0,
+    ),
+    axis=1,
+)
 
 
 def slope(z):
@@ -34,7 +43,7 @@
     width = first_weight.shape[1]
     kinds = head_weight.shape[0] // PP
     rows_first, rows_second = (
-        lax.all_to_all(first_weight, "tensor", split_axis=0, concat_axis=1, tiled=True),
+        balance_ports(first_weight, "tensor"),
         lax.all_to_all(second_weight, "tensor", split_axis=0, concat_axis=1, tiled=True),
     )
     head_cols = lax.all_to_all(head_weight, "tensor", split_axis=1, concat_axis=0, tiled=True)

time: 391 us -> 390 us (level)
  waiting for transfers between devices: 245 us -> 227 us
  blocking collectives: 69.1 us -> 83.8 us
    all_to_all x1, waiting for transfers between devices: 22.4 us -> 0.01 us  [lax.all_to_all(jnp.stack(jnp.split(point, lax.axis_size(device_axis), axi...]
    psum x1, blocking collectives: 5.57 us -> 20.4 us  [per_device(): loss = lax.psum(jnp.sum(root), 'tensor') / V]
    unnamed x8, waiting for transfers between devices: 66.7 us -> 71.6 us
  transfers between devices with their start and end apart: 9 -> 9, of which waited for: 7 -> 6; matrix products, arithmetic and copies ran while one was open for 7% -> 7% of each run, Pallas kernels for 0% -> 0%
where the time goes in v1:
time: 390 us
  waiting for transfers between devices  227 us (58%)
  blocking collectives  83.8 us (21%)
  matrix products  36.5 us (9%)
  between operations  16.8 us (4%)
  local copies, waits for them, and re-layouts  11.9 us (3%)
  starting transfers between devices  8.01 us (2%)
  other arithmetic  5.44 us (1%)
    unnamed x8, waiting for transfers between devices  71.6 us
    reduce_scatter x1, waiting for transfers between devices, per_device(): lax.psum_scatter(head_term, 'space', scatter_dimension=1, tiled=True)  59.1 us
    all_gather x1, waiting for transfers between devices, per_device(): full_in = lax.all_gather(tokens, 'tensor', axis=1, tiled=True)  34.5 us
    psum x1, blocking collectives, per_device(): error_sum = lax.psum(local_error, 'space')  33.2 us
    all_gather x1, waiting for transfers between devices, per_device(): full_one = lax.all_gather(hidden_one, 'tensor', axis=1, tiled=True)  30.2 us
    all_gather x1, waiting for transfers between devices, per_device(): full_two = lax.all_gather(hidden_two, 'tensor', axis=1, tiled=True)  23.1 us
    all_to_all x1, blocking collectives, per_device(): lax.all_to_all(second_weight, 'tensor', split_axis=0, concat_axis=1, tile...  22.7 us
    psum x1, blocking collectives, per_device(): loss = lax.psum(jnp.sum(root), 'tensor') / V  20.4 us
  transfers between devices with their start and end apart: 9, of which 6 were waited for; matrix products, arithmetic and copies ran while one was open for 7% of the time, Pallas kernels for 0%

profile of v1, /device:TPU:0, one launch (start us, length us, event | category | flops | bytes accessed | tf_op | source)
XLA Modules:
  0.0 389.6 jit_solution(16165921942225958069)
XLA Ops:
  7.2 0.7 all-gather.6.cloned.1.call-update
  8.0 34.5 %all-gather.6.cloned.1.call-done = bf16[896,1024]{1,0:T(8,128)(2,1)} async-done(((bf16[896,512]{1,0:T(8,128)(2,1)}), bf16[896,1024]{1,0:T(8,128)(2,1)}) %all-gather.6.cloned.1.call-update) | async-done | bytes 1835024 | tf_op jit(solution)/shard_map/all_gather | solution.py:61
  42.4 8.0 %fusion.2 = (bf16[896,512]{1,0:T(8,128)(2,1)}, f32[896,512]{1,0:T(8,128)}) fusion(bf16[896,1024]{1,0:T(8,128)(2,1)} %all-gather.6.cloned.1.call-done, bf16[1024,512]{1,0:T(8,128)(2,1)} %param.9), kind=kOutput, calls=%fused_computation.7 | convolution fusion | flops 969342976 | bytes 5636096 | tf_op jit(solution)/shard_map/dot_general | solution.py:62
  50.5 30.2 %all-gather.8.cloned.1.call-done = bf16[896,1024]{1,0:T(8,128)(2,1)} async-done(((bf16[896,512]{1,0:T(8,128)(2,1)}), bf16[896,1024]{1,0:T(8,128)(2,1)}) %all-gather.8.cloned.1.call-update) | async-done | bytes 1835024 | tf_op jit(solution)/shard_map/all_gather | solution.py:64
  80.7 7.5 %fusion.5 = (bf16[896,512]{1,0:T(8,128)(2,1)}, f32[896,512]{1,0:T(8,128)}) fusion(bf16[896,1024]{1,0:T(8,128)(2,1)} %all-gather.8.cloned.1.call-done, bf16[1024,512]{1,0:T(8,128)(2,1)S(1)} %copy-done.4), kind=kOutput, calls=%fused_computation.10 | convolution fusion | flops 969342976 | bytes 5636096 | tf_op jit(solution)/shard_map/dot_general | solution.py:65
  88.2 0.8 copy.39
  89.0 4.1 %all-to-all-start = ((bf16[176,2,512]{2,0,1:T(8,128)(2,1)}), bf16[176,2,512]{2,0,1:T(8,128)(2,1)}, u32[]{:S(2)}, u32[]{:S(2)}) async-start(bf16[176,2,512]{2,0,1:T(8,128)(2,1)} %bitcast.39), calls=%async_computation | async-start | bytes 720896 | tf_op jit(solution)/shard_map/all_to_all | solution.py:49
  93.9 0.2 broadcast_in_dim.69
  95.5 0.8 multiply_reduce_fusion
  96.2 23.1 %all-gather.10.cloned.1.call-done = bf16[896,1024]{1,0:T(8,128)(2,1)} async-done(((bf16[896,512]{1,0:T(8,128)(2,1)}), bf16[896,1024]{1,0:T(8,128)(2,1)}) %all-gather.10.cloned.1.call-update) | async-done | bytes 1835024 | tf_op jit(solution)/shard_map/all_gather | solution.py:67
  119.4 2.6 fusion.33
  122.2 33.2 %all-reduce = (f32[44]{0:T(128)S(1)}, f32[44]{0:T(128)S(1)}) all-reduce(f32[44]{0:T(128)S(1)} %reduce_sum.36, f32[44]{0:T(128)S(1)} %multiply_reduce_fusion), channel_id=1, replica_groups=mesh['space'=16,'tensor'=2] {'space'}, use_global_device_ids=true, to_apply=%region_2.3 | all-reduce | flops 88 | bytes 704 | tf_op jit(solution)/shard_map/psum | solution.py:73
  155.7 7.6 %all_gather.21 = bf16[352,896]{1,0:T(8,128)(2,1)S(1)} all-gather(bf16[176,896]{1,0:T(8,128)(2,1)S(1)} %multiply_convert_fusion), channel_id=1, replica_groups=mesh['space'=16,'tensor'=2] {'tensor'}, dimensions={0}, use_global_device_ids=true | all-gather | bytes 946176 | tf_op jit(solution)/shard_map/all_gather | solution.py:80
  163.4 3.7 fusion.11
  167.2 22.7 %all_to_all.43 = bf16[2,512,512]{2,1,0:T(8,128)(2,1)S(1)} all-to-all(bf16[2,512,512]{2,1,0:T(8,128)(2,1)S(1)} %bitcast.44), channel_id=1, replica_groups=mesh['space'=16,'tensor'=2] {'tensor'}, dimensions={0} | all-to-all | bytes 2097152 | tf_op jit(solution)/shard_map/all_to_all | solution.py:47
  189.8 0.5 copy.26
  190.4 8.6 %all-gather.12.cloned.1.call-done = bf16[896,1024]{1,0:T(8,128)(2,1)} async-done(((bf16[896,512]{1,0:T(8,128)(2,1)}), bf16[896,1024]{1,0:T(8,128)(2,1)}) %all-gather.12.cloned.1.call-update) | async-done | bytes 1835024 | tf_op jit(solution)/shard_map/all_gather | solution.py:84
  198.9 4.6 %fusion.17 = bf16[896,512]{1,0:T(8,128)(2,1)} fusion(f32[896,512]{1,0:T(8,128)} %get-tuple-element.38, bf16[896,1024]{1,0:T(8,128)(2,1)} %all-gather.12.cloned.1.call-done, bf16[512,1024]{0,1:T(8,128)(2,1)S(1)} %bitcast.46), kind=kOutput, calls=%fused_computation.22 | convolution fusion | flops 944111616 | bytes 5636096 | tf_op jit(solution)/shard_map/dot_general | solution.py:28
  203.6 3.2 fusion.39
  206.8 1.3 convolution_bitcast_fusion
  208.1 2.5 pad_maximum_fusion
  210.6 5.5 %copy.31 = f32[1024,1024]{1,0:T(8,128)} copy(f32[1024,1024]{0,1:T(8,128)} %pad_maximum_fusion) | data formatting | bytes 8388608
  216.2 1.2 copy-done.6
  217.9 1.1 pad_maximum_fusion.1
  218.9 3.6 all-to-all-start.2
  222.6 1.9 fusion.40
  224.5 0.6 reduce_sum.38
  225.1 20.4 %psum.23 = f32[]{:T(128)} all-reduce(f32[]{:T(128)} %reduce_sum.38), channel_id=1, replica_groups=mesh['space'=16,'tensor'=2] {'tensor'}, use_global_device_ids=true, to_apply=%region_6.7 | all-reduce | flops 1 | bytes 8 | tf_op jit(solution)/shard_map/psum | solution.py:75
  246.1 3.9 fusion.38
  250.0 70.8 %reduce-scatter.7.cloned.1.call-done = f32[64,1024]{1,0:T(8,128)} async-done(((f32[1024,1024]{1,0:T(8,128)}), f32[64,1024]{1,0:T(8,128)}) %reduce-scatter.7.cloned.1.call-update) | async-done | bytes 262160
  320.8 1.7 fusion.37
  322.5 59.1 %reduce-scatter.5.cloned.1.call-done = f32[176,64]{0,1:T(8,128)} async-done(((f32[176,1024]{0,1:T(8,128)}), f32[176,64]{0,1:T(8,128)}) %reduce-scatter.5.cloned.1.call-update) | async-done | bytes 45072 | tf_op jit(solution)/shard_map/reduce_scatter | solution.py:82
  (56 shorter events, 2.8 us)
Async XLA Ops:
  7.2 35.2 %all-gather.6.cloned.1.call-start = ((), (), s32[]{:S(2)}) async-start(), calls=%async_computation.5 | async-start | bytes 2752512 | tf_op jit(solution)/shard_map/all_gather | solution.py:61
  7.9 72.8 %copy-start.4 = (bf16[1024,512]{1,0:T(8,128)(2,1)S(1)}, bf16[1024,512]{1,0:T(8,128)(2,1)}, u32[]{:S(2)}) copy-start(bf16[1024,512]{1,0:T(8,128)(2,1)} %param.10) | copy-start | bytes 3145732
  7.9 72.8 %all-gather.8.cloned.1.call-start = ((), (), s32[]{:S(2)}) async-start(), calls=%async_computation.6 | async-start | bytes 2752512 | tf_op jit(solution)/shard_map/all_gather | solution.py:64
  50.4 37.8 %copy-start.3 = (bf16[176,1024]{1,0:T(8,128)(2,1)S(1)}, bf16[176,1024]{1,0:T(8,128)(2,1)}, u32[]{:S(2)}) copy-start(bf16[176,1024]{1,0:T(8,128)(2,1)} %param.11) | copy-start | bytes 1081348
  50.4 68.9 %all-gather.10.cloned.1.call-start = ((), (), s32[]{:S(2)}) async-start(), calls=%async_computation.7 | async-start | bytes 2752512 | tf_op jit(solution)/shard_map/all_gather | solution.py:67
  88.2 5.0 %copy-start.7 = (s32[4,896]{1,0:T(4,128)S(1)}, s32[4,896]{1,0:T(4,128)}, u32[]{:S(2)}) copy-start(s32[4,896]{1,0:T(4,128)} %param.13) | copy-start | bytes 43012
  89.0 74.4 %all-to-all-start = ((bf16[176,2,512]{2,0,1:T(8,128)(2,1)}), bf16[176,2,512]{2,0,1:T(8,128)(2,1)}, u32[]{:S(2)}, u32[]{:S(2)}) async-start(bf16[176,2,512]{2,0,1:T(8,128)(2,1)} %bitcast.39), calls=%async_computation | async-start | bytes 720896 | tf_op jit(solution)/shard_map/all_to_all | solution.py:49
  93.1 105.8 %all-gather.12.cloned.1.call-start = ((), (), s32[]{:S(2)}) async-start(), calls=%async_computation.8 | async-start | bytes 2752512 | tf_op jit(solution)/shard_map/all_gather | solution.py:84
  93.8 0.7 copy-start.8
  163.4 3.8 copy-start.5
  167.1 79.0 %all-gather.14.cloned.1.call-start = ((), (), s32[]{:S(2)}) async-start(), calls=%async_computation.9 | async-start | bytes 2752512 | tf_op jit(solution)/shard_map/all_gather | solution.py:104
  203.6 3.2 copy-start.1
  203.6 3.2 copy-start.2
  203.6 117.2 %reduce-scatter.7.cloned.1.call-start = ((), (), s32[]{:S(2)}) async-start(), calls=%async_computation.11 | async-start | bytes 4456448
  216.1 1.2 copy-start.6
  217.9 4.7 %copy-start = (bf16[896,1024]{1,0:T(8,128)(2,1)S(1)}, bf16[896,1024]{1,0:T(8,128)(2,1)}, u32[]{:S(2)}) copy-start(bf16[896,1024]{1,0:T(8,128)(2,1)} %all-gather.10.cloned.1.call-done) | copy-start | bytes 5505028
  218.9 27.1 %all-to-all-start.2 = ((bf16[2,512,512]{1,2,0:T(8,128)(2,1)}), bf16[2,512,512]{1,2,0:T(8,128)(2,1)S(1)}, u32[]{:S(2)}, u32[]{:S(2)}) async-start(bf16[2,512,512]{1,2,0:T(8,128)(2,1)} %pad_maximum_fusion.1), calls=%async_computation.2 | async-start | bytes 2097152 | tf_op jit(solution)/shard_map/all_to_all | solution.py:12
  222.5 159.1 %reduce-scatter.5.cloned.1.call-start = ((), (), s32[]{:S(2)}) async-start(), calls=%async_computation.10 | async-start | bytes 1114112 | tf_op jit(solution)/shard_map/reduce_scatter | solution.py:82
Sparse Core Ops, SparseCore 0:
  9.5 32.8 all-gather.5
  50.5 30.1 all-gather.7
  88.3 30.9 all-gather.9
  167.2 31.6 all-gather.11
  203.7 38.3 all-gather.13
  245.8 74.9 reduce-scatter.6
  325.0 56.5 reduce-scatter.4
